TPU v7x, 512 devices: a 4x2x32 block of a 4x8x32 slice. The times are simulated.
512 devices in a mesh: groups: 2 (over y), expert: 32 (over z), tensor: 8 (over x, core).
Axes of the slice: x: 4, y: 2, z: 32, core: 2. Of those that a mesh axis runs over, the one named last changes fastest.
The devices are a block of a 4x8x32 slice.
Arguments:
- tokens: bfloat16 [8192, 7168], P(('groups', 'expert'), 'tensor'), parts along dimension 0, may hold values from -6 to 6
- choices: int32 [8192, 4], P(('groups', 'expert')), parts along dimension 0, may hold values from 0 to 15, all different within a row; in each aligned block of 128 rows (0 to 127, 128 to 255, ...) at most 48 rows name the same one
- affinity: float32 [8192, 4], P(('groups', 'expert')), parts along dimension 0, may hold values from -6 to 6
- expert_gate: bfloat16 [7168, 16384], P('tensor', 'expert'), may hold values from -0.0625 to 0.0625
- expert_up: bfloat16 [7168, 16384], P('tensor', 'expert'), may hold values from -0.0625 to 0.0625
- expert_down: bfloat16 [16384, 7168], P('expert', 'tensor'), may hold values from -0.1875 to 0.1875
- shared_in: bfloat16 [2, 1024, 7168], P(None, 'expert', 'tensor'), may hold values from -0.0625 to 0.0625
- shared_down: bfloat16 [1024, 7168], P('expert', 'tensor'), may hold values from -0.1875 to 0.1875
Outputs:
- mixed: bfloat16 [8192, 7168], P(('groups', 'expert'), 'tensor'), parts along dimension 0
There are 2 independent parts, one for each index of `groups`. A program takes and returns all parts, laid end to end along the dimension named above; an argument that names none is the same for every part. Nothing has to cross between parts.
Inputs may be any that keep to these rules, and one draw needn't show every extreme that they name: `choices`: within the rows of one index of expert (128 tokens) every expert is named at most 48 times, a bound that some block reaches; a token names 4 different experts.
All inputs are finite; a program needn't handle non-finite values.
Results may differ from a plain program's by a relative error of at most 0.02.
Values may be sent and summed in bfloat16 or wider, within the bound.
No kernel may reach another device: no remote copies, remote signals or barrier semaphores. Data moves between devices by JAX's collectives and lax.ppermute only.
A program may use at most 64 MiB of HBM per device.

v0:
```python
import jax
import jax.numpy as jnp
from jax import lax
from jax.sharding import PartitionSpec as P

FFE = 1024
EXPERTS = 16
TOP = 4
CAP = 48


def local(tokens, choices, affinity, expert_gate, expert_up, expert_down, shared_in, shared_down):
    tok_rows = tokens.shape[0]
    width_slice = tokens.shape[1]
    expert_count = lax.axis_size("expert")
    column_count = expert_gate.shape[1]
    piece_width = min(FFE, column_count)
    local_count = column_count // piece_width
    split_count = FFE // piece_width
    sigmoids = jax.nn.sigmoid(affinity)
    mix = 2.5 * sigmoids / jnp.sum(sigmoids, axis=1, keepdims=True)
    flat_ids = choices.reshape(-1)
    onehot = (flat_ids[:, None] == jnp.arange(EXPERTS, dtype=jnp.int32)[None, :]).astype(jnp.int32)
    earlier = jnp.cumsum(onehot, axis=0) - onehot
    position = jnp.sum(earlier * onehot, axis=1)
    slot_ids = flat_ids * CAP + position
    row_owner = jnp.arange(tok_rows * TOP, dtype=jnp.int32) // TOP
    source_row = jnp.zeros((EXPERTS * CAP,), jnp.int32).at[slot_ids].set(row_owner)
    filled = jnp.zeros((EXPERTS * CAP,), jnp.int32).at[slot_ids].set(1)
    packed = jnp.where(filled[:, None] > 0, tokens[source_row], jnp.zeros((), jnp.bfloat16))
    outbound = jnp.broadcast_to(
        packed.reshape(EXPERTS, 1, CAP, width_slice), (EXPERTS, split_count, CAP, width_slice)
    )
    outbound = outbound.reshape(expert_count, local_count, CAP, width_slice)
    gate_cols = expert_gate.reshape(width_slice, local_count, piece_width)
    up_cols = expert_up.reshape(width_slice, local_count, piece_width)
    down_rows = expert_down.reshape(local_count, piece_width, width_slice)
    received = lax.all_to_all(outbound, "expert", split_axis=0, concat_axis=0, tiled=True)
    gate_part = jnp.einsum(
        "nlcd,dlp->nlcp", received, gate_cols, preferred_element_type=jnp.float32
    )
    up_part = jnp.einsum("nlcd,dlp->nlcp", received, up_cols, preferred_element_type=jnp.float32)
    gate_sum = lax.psum(gate_part.astype(jnp.bfloat16), "tensor").astype(jnp.float32)
    up_sum = lax.psum(up_part.astype(jnp.bfloat16), "tensor").astype(jnp.float32)
    hidden = (jax.nn.silu(gate_sum) * up_sum).astype(jnp.bfloat16)
    produced = jnp.einsum("nlcp,lpd->nlcd", hidden, down_rows, preferred_element_type=jnp.float32)
    returned = lax.all_to_all(
        produced.astype(jnp.bfloat16), "expert", split_axis=0, concat_axis=0, tiled=True
    )
    summed = jnp.sum(
        returned.astype(jnp.float32).reshape(EXPERTS, split_count, CAP, width_slice), axis=1
    )
    picked = summed.reshape(EXPERTS * CAP, width_slice)[slot_ids].reshape(
        tok_rows, TOP, width_slice
    )
    routed = jnp.sum(mix[:, :, None] * picked, axis=1)
    terms = jnp.einsum(
        "td,gnd->gtn",
        tokens,
        lax.all_gather(shared_in, "expert", axis=1, tiled=True),
        preferred_element_type=jnp.float32,
    )
    sums = lax.psum(terms.astype(jnp.bfloat16), "tensor").astype(jnp.float32)
    shared_hidden = (jax.nn.silu(sums[0]) * sums[1]).astype(jnp.bfloat16)
    shared_out = jnp.dot(
        shared_hidden,
        lax.all_gather(shared_down, "expert", axis=0, tiled=True),
        preferred_element_type=jnp.float32,
    )
    return (routed + shared_out).astype(jnp.bfloat16)


def solution(mesh):
    placed = (
        P(("groups", "expert"), "tensor"),
        P(("groups", "expert"), None),
        P(("groups", "expert"), None),
        P("tensor", "expert"),
        P("tensor", "expert"),
        P("expert", "tensor"),
        P(None, "expert", "tensor"),
        P("expert", "tensor"),
    )
    return jax.shard_map(
        local,
        mesh=mesh,
        in_specs=placed,
        out_specs=P(("groups", "expert"), "tensor"),
        check_vma=False,
    )
```

profile of v0, /device:TPU:96, one launch (start us, length us, event | category | flops | bytes accessed | tf_op | source)
XLA Modules:
  0.0 806.6 jit_solution(5608995960913174588)
XLA Ops:
  6.6 0.9 copy.17
  7.6 0.7 broadcast_multiply_fusion
  8.3 1.2 reduce-window.6
  10.1 2.4 scatter_custom_fusion.1
  12.6 2.4 scatter_custom_fusion
  15.1 2.8 gather_fusion
  18.2 1.8 broadcast_in_dim.37
  20.0 44.3 %all-to-all-start = ((bf16[32,1,48,896]{3,2,1,0:T(8,128)(2,1)}), bf16[32,1,48,896]{3,2,1,0:T(8,128)(2,1)}, u32[]{:S(2)}, u32[]{:S(2)}) async-start(bf16[32,1,48,896]{3,2,1,0:T(8,128)(2,1)} %bitcast.93), calls=%async_computation | async-start | bytes 5505024 | tf_op jit(solution)/shard_map/all_to_all | solution.py:38
  64.4 0.7 all-gather.3.cloned.1.call-update
  65.2 305.2 %all-gather.3.cloned.1.call-done = bf16[2,1024,896]{2,1,0:T(8,128)(2,1)} async-done(((bf16[2,32,896]{2,1,0:T(8,128)(2,1)}), bf16[2,1024,896]{2,1,0:T(8,128)(2,1)}) %all-gather.3.cloned.1.call-update) | async-done | bytes 3670032 | tf_op jit(solution)/shard_map/all_gather | solution.py:60
  370.4 4.0 fusion.23
  374.4 4.8 fusion.17
  379.2 4.7 fusion.20
  384.0 99.2 %all-reduce.3.cloned.1.call-done = (bf16[32,1,48,512]{3,2,0,1:T(8,128)(2,1)}, bf16[32,1,48,512]{3,2,0,1:T(8,128)(2,1)}, bf16[2,128,1024]{1,2,0:T(8,128)(2,1)}) async-done(((bf16[32,1,48,512]{3,2,0,1:T(8,128)(2,1)}, bf16[32,1,48,512]{3,2,0,1:T(8,128)(2,1)}, bf16[2,128,1024]{1,2,0:T(8,128)(2,1)}), (bf16[32,1,48,512]{3,2,0,1:T(8,128)(2,1)}, bf16[32,1,48,512]{3,2,0,1:T(8,128)(2,1)}, ...) | async-done | bytes 3670032 | tf_op jit(solution)/shard_map/psum | solution.py:44
  483.2 5.5 convert_bitcast_fusion
  488.7 23.4 %all-to-all-start.1 = ((bf16[32,1,48,896]{3,2,1,0:T(8,128)(2,1)}), bf16[32,1,48,896]{3,2,1,0:T(8,128)(2,1)}, u32[]{:S(2)}, u32[]{:S(2)}) async-start(bf16[32,1,48,896]{3,2,1,0:T(8,128)(2,1)} %convert_bitcast_fusion), calls=%async_computation.1 | async-start | bytes 5505024 | tf_op jit(solution)/shard_map/all_to_all | solution.py:47
  512.3 0.5 all-gather.5.cloned.1.call-update
  513.1 1.0 convert_element_type.87
  514.1 270.0 %all-to-all-done.1 = bf16[32,1,48,896]{3,2,1,0:T(8,128)(2,1)} async-done(((bf16[32,1,48,896]{3,2,1,0:T(8,128)(2,1)}), bf16[32,1,48,896]{3,2,1,0:T(8,128)(2,1)}, u32[]{:S(2)}, u32[]{:S(2)}) %all-to-all-start.1) | async-done | bytes 2752544 | tf_op jit(solution)/shard_map/all_to_all | solution.py:47
  784.1 4.0 convert_reduce_fusion
  788.2 4.4 gather_fusion.1
  792.6 1.8 reshape.107
  794.4 2.7 multiply_reduce_fusion
  797.1 3.0 fusion.24
  (39 shorter events, 1.8 us)
Async XLA Ops:
  6.5 476.6 %copy-start = (bf16[512,896]{1,0:T(8,128)(2,1)S(1)}, bf16[512,896]{1,0:T(8,128)(2,1)}, u32[]{:S(2)}) copy-start(bf16[512,896]{1,0:T(8,128)(2,1)} %param.13) | copy-start | bytes 2752516
  6.6 8.6 %copy-start.1 = (bf16[128,896]{1,0:T(8,128)(2,1)S(1)}, bf16[128,896]{1,0:T(8,128)(2,1)}, u32[]{:S(2)}) copy-start(bf16[128,896]{1,0:T(8,128)(2,1)} %param.8) | copy-start | bytes 688132
  20.0 354.4 %all-to-all-start = ((bf16[32,1,48,896]{3,2,1,0:T(8,128)(2,1)}), bf16[32,1,48,896]{3,2,1,0:T(8,128)(2,1)}, u32[]{:S(2)}, u32[]{:S(2)}) async-start(bf16[32,1,48,896]{3,2,1,0:T(8,128)(2,1)} %bitcast.93), calls=%async_computation | async-start | bytes 5505024 | tf_op jit(solution)/shard_map/all_to_all | solution.py:38
  64.3 310.0 %copy-start.4 = (bf16[896,512]{1,0:T(8,128)(2,1)S(1)}, bf16[896,512]{1,0:T(8,128)(2,1)}, u32[]{:S(2)}) copy-start(bf16[896,512]{1,0:T(8,128)(2,1)} %param.12) | copy-start | bytes 2752516
  64.3 306.1 %all-gather.3.cloned.1.call-start = ((), (), s32[]{:S(2)}) async-start(), calls=%async_computation.2 | async-start | bytes 3784704 | tf_op jit(solution)/shard_map/all_gather | solution.py:60
  65.1 418.0 %all-reduce.3.cloned.1.call-start = ((), (), s32[]{:S(2)}) async-start(), calls=%async_computation.4 | async-start | bytes 7340032 | tf_op jit(solution)/shard_map/psum | solution.py:44
  374.4 4.8 copy-start.5
  488.7 24.2 %copy-start.3 = (f32[128,4]{0,1:T(4,128)S(1)}, f32[128,4]{0,1:T(4,128)}, u32[]{:S(2)}) copy-start(f32[128,4]{0,1:T(4,128)} %param.10) | copy-start | bytes 6148
  488.7 24.4 %copy-start.2 = (bf16[2,128,1024]{1,2,0:T(8,128)(2,1)S(1)}, bf16[2,128,1024]{1,2,0:T(8,128)(2,1)}, u32[]{:S(2)}) copy-start(bf16[2,128,1024]{1,2,0:T(8,128)(2,1)} %get-tuple-element.7) | copy-start | bytes 1572868
  488.7 295.4 %all-to-all-start.1 = ((bf16[32,1,48,896]{3,2,1,0:T(8,128)(2,1)}), bf16[32,1,48,896]{3,2,1,0:T(8,128)(2,1)}, u32[]{:S(2)}, u32[]{:S(2)}) async-start(bf16[32,1,48,896]{3,2,1,0:T(8,128)(2,1)} %convert_bitcast_fusion), calls=%async_computation.1 | async-start | bytes 5505024 | tf_op jit(solution)/shard_map/all_to_all | solution.py:47
  512.1 285.0 %all-gather.5.cloned.1.call-start = ((), (), s32[]{:S(2)}) async-start(), calls=%async_computation.3 | async-start | bytes 1892352 | tf_op jit(solution)/shard_map/all_gather | solution.py:67
Sparse Core Ops, SparseCore 0:
  67.3 303.0 all-gather.2
  384.1 99.0 all-reduce.2
  515.0 246.0 all-gather.4
where the time goes:
time: 807 us
  waiting for transfers between devices  676 us (84%)
  starting transfers between devices  68.1 us (8%)
  matrix products  22 us (3%)
  local copies, waits for them, and re-layouts  17.5 us (2%)
  between operations  13.3 us (2%)
  other arithmetic  10 us (1%)
    all_gather x1, waiting for transfers between devices, local(): lax.all_gather(shared_in, 'expert', axis=1, tiled=True)  305 us
    all_to_all x1, waiting for transfers between devices, local(): lax.all_to_all(produced.astype(jnp.bfloat16), 'expert', split_axis=0, con...  270 us
    psum x1, waiting for transfers between devices, local(): lax.psum(up_part.astype(jnp.bfloat16), 'tensor').astype(jnp.float32)  99.2 us
    all_to_all x1, starting transfers between devices, local(): lax.all_to_all(outbound, 'expert', split_axis=0, concat_axis=0, tiled=True)  44.3 us
    all_to_all x1, starting transfers between devices, local(): lax.all_to_all(produced.astype(jnp.bfloat16), 'expert', split_axis=0, con...  23.4 us
  transfers between devices with their start and end apart: 5, of which 3 were waited for; matrix products, arithmetic and copies ran while one was open for 2% of the time, Pallas kernels for 0%

commit v1 on v0

v1 whole, which is shorter than its diff:
```python
import jax
import jax.numpy as jnp
from jax import lax
from jax.sharding import PartitionSpec as P

FFE = 1024
CAP = 48
BF = jnp.bfloat16
F32 = jnp.float32


def dot(spec, a, b):
    return jnp.einsum(spec, a, b, preferred_element_type=F32)


def route(info, columns, top):
    count, _, tok = info.shape
    own = (lax.axis_index("expert") * columns // FFE).astype(F32)
    hit = info[:, :top, :] == own
    named = jnp.any(hit, axis=1)
    weight = jnp.sum(jnp.where(hit, info[:, top:, :], 0.0), axis=1)
    order = jnp.arange(tok)
    before = (order[:, None] < order[None, :]).astype(BF)
    position = dot("ns,st->nt", named.astype(BF), before).astype(jnp.int32)
    slots = jnp.arange(CAP, dtype=jnp.int32)[None, :, None]
    picks = named[:, None, :] & (position[:, None, :] == slots)
    slot_weight = jnp.sum(jnp.where(picks, weight[:, None, :], 0.0), axis=2)
    return picks.astype(BF), slot_weight


def local(tokens, choices, affinity, expert_gate, expert_up, expert_down, shared_in, shared_down):
    tok, width = tokens.shape
    blocks = lax.axis_size("expert")
    parts = lax.axis_size("tensor")
    columns = expert_gate.shape[1]
    units = shared_in.shape[1]
    top = choices.shape[1]
    total = blocks * tok
    sigmoids = jax.nn.sigmoid(affinity)
    mix = 2.5 * sigmoids / jnp.sum(sigmoids, axis=1, keepdims=True)
    info = jnp.concatenate([choices.astype(F32).T, mix.T], axis=0)
    info = lax.all_gather(info, "expert", axis=0)
    picks, slot_weight = route(info, columns, top)
    everyone = lax.all_gather(tokens, "expert", axis=0, tiled=True)
    received = dot("nct,ntd->ncd", picks, everyone.reshape(blocks, tok, width)).astype(BF)
    received = received.reshape(parts, blocks * CAP // parts, width)
    gate = dot("jrd,dp->jrp", received, expert_gate).astype(BF)
    up = dot("jrd,dp->jrp", received, expert_up).astype(BF)
    shared = dot("hd,td->ht", shared_in.reshape(2 * units, width), everyone).astype(BF)
    shared = shared.reshape(2 * units, parts, total // parts).transpose(1, 0, 2)
    slots = blocks * CAP // parts
    sums = lax.psum_scatter(
        jnp.concatenate([gate, up, shared], axis=1), "tensor", scatter_dimension=0, tiled=True
    )[0].astype(F32)
    gates = jnp.concatenate([sums[:slots], sums[2 * slots : 2 * slots + units]], axis=0)
    ups = jnp.concatenate([sums[slots : 2 * slots], sums[2 * slots + units :]], axis=0)
    hidden = (jax.nn.silu(gates) * ups).astype(BF)
    hidden = lax.all_gather(hidden, "tensor", axis=0)
    shared_hidden = hidden[:, slots:].reshape(parts, units, blocks // parts, tok)
    shared_hidden = shared_hidden.transpose(0, 2, 1, 3).reshape(blocks, units, tok)
    produced = dot("rp,pd->rd", hidden[:, :slots].reshape(blocks * CAP, columns), expert_down)
    produced = (produced.reshape(blocks, CAP, width) * slot_weight[:, :, None]).astype(BF)
    values = jnp.concatenate(
        [produced, jnp.broadcast_to(shared_down[None], (blocks, units, width))], axis=1
    )
    share = dot("nkt,nkd->ntd", jnp.concatenate([picks, shared_hidden], axis=1), values)
    return lax.psum_scatter(
        share.astype(BF).reshape(total, width), "expert", scatter_dimension=0, tiled=True
    )


def solution(mesh):
    placed = (
        P(("groups", "expert"), "tensor"),
        P(("groups", "expert"), None),
        P(("groups", "expert"), None),
        P("tensor", "expert"),
        P("tensor", "expert"),
        P("expert", "tensor"),
        P(None, "expert", "tensor"),
        P("expert", "tensor"),
    )
    return jax.shard_map(
        local,
        mesh=mesh,
        in_specs=placed,
        out_specs=P(("groups", "expert"), "tensor"),
        check_vma=False,
    )
```

time: 807 us -> 451 us (0.56)
  the two profiles are of different devices: /device:TPU:96 before, /device:TPU:36 now
where the time goes in v1:
time: 451 us
  waiting for transfers between devices  316 us (70%)
  blocking collectives  95.5 us (21%)
  matrix products  16.6 us (4%)
  between operations  13.3 us (3%)
  other arithmetic  5.51 us (1%)
    reduce_scatter x1, waiting for transfers between devices, local(): lax.psum_scatter(share.astype(BF).reshape(total, width), 'expert', scatte...  154 us
    all_gather x1, blocking collectives, local(): info = lax.all_gather(info, 'expert', axis=0)  95.5 us
    all_gather x1, waiting for transfers between devices, local(): everyone = lax.all_gather(tokens, 'expert', axis=0, tiled=True)  78.3 us
    all_gather x1, waiting for transfers between devices, local(): hidden = lax.all_gather(hidden, 'tensor', axis=0)  43.5 us
    reduce_scatter x1, waiting for transfers between devices, local(): lax.psum_scatter(jnp.concatenate([gate, up, shared], axis=1), 'tensor', s...  39.6 us
    dot_general x7, matrix products, dot(): return jnp.einsum(spec, a, b, preferred_element_type=F32)  16.6 us
  transfers between devices with their start and end apart: 4, of which 4 were waited for; matrix products, arithmetic and copies ran while one was open for 1% of the time, Pallas kernels for 0%

profile of v1, /device:TPU:36, one launch (start us, length us, event | category | flops | bytes accessed | tf_op | source)
XLA Modules:
  0.0 450.5 jit_solution(9961993956879836516)
XLA Ops:
  6.6 0.7 all-gather.4.cloned.1.call-update
  7.4 0.7 fusion.17
  8.1 0.7 convert_bitcast_fusion
  8.8 0.7 divide_bitcast_fusion
  9.5 95.5 %all-gather = f32[256,128]{1,0:T(8,128)S(1)} all-gather(f32[8,128]{1,0:T(8,128)S(1)} %pad_maximum_fusion.3), channel_id=2, replica_groups=mesh['groups'=2,'expert'=32,'tensor'=8] {'expert'}, dimensions={0}, use_global_device_ids=true | all-gather | bytes 135168 | tf_op jit(solution)/shard_map/all_gather | solution.py:42
  105.1 0.1 convolution_convert_fusion.5
  105.2 78.3 %all-gather.4.cloned.1.call-done = bf16[4096,896]{1,0:T(8,128)(2,1)} async-done(((bf16[128,896]{1,0:T(8,128)(2,1)}), bf16[4096,896]{1,0:T(8,128)(2,1)}) %all-gather.4.cloned.1.call-update) | async-done | bytes 7340048 | tf_op jit(solution)/shard_map/all_gather | solution.py:44
  183.5 5.6 %convolution_convert_fusion.1 = bf16[64,4096]{1,0:T(8,128)(2,1)S(1)} fusion(bf16[64,896]{1,0:T(8,128)(2,1)} %bitcast.44, bf16[4096,896]{1,0:T(8,128)(2,1)} %all-gather.4.cloned.1.call-done), kind=kOutput, calls=%fused_computation.2 | convolution fusion | flops 470024192 | bytes 7979008 | tf_op jit(solution)/shard_map/hd,td->ht/dot_general | solution.py:13
  189.2 1.2 convolution_convert_fusion.2
  190.5 1.8 convolution_convert_fusion.3
  192.3 1.8 convolution_convert_fusion.4
  194.1 1.9 pad_maximum_fusion
  196.2 39.6 %reduce-scatter.3.cloned.1.call-done = bf16[1,448,512]{2,1,0:T(8,128)(2,1)} async-done(((bf16[8,448,512]{2,1,0:T(8,128)(2,1)}), bf16[1,448,512]{2,1,0:T(8,128)(2,1)}) %reduce-scatter.3.cloned.1.call-update) | async-done | bytes 458768 | tf_op jit(solution)/shard_map/reduce_scatter | solution.py:52
  235.8 0.8 fusion.21
  236.6 1.1 fusion.20
  237.7 0.8 fusion.12
  238.7 0.3 select_reduce_fusion
  239.0 0.2 fusion.8
  239.2 43.5 %all-gather.6.cloned.1.call-done = bf16[8,224,512]{2,1,0:T(8,128)(2,1)} async-done(((bf16[1,224,512]{2,1,0:T(8,128)(2,1)}), bf16[8,224,512]{2,1,0:T(8,128)(2,1)}) %all-gather.6.cloned.1.call-update) | async-done | bytes 1835024 | tf_op jit(solution)/shard_map/all_gather | solution.py:58
  282.7 1.4 slice-done
  284.1 1.8 multiply_convert_fusion
  286.0 0.1 broadcast_in_dim.21
  286.1 4.2 convolution_convert_fusion
  290.4 153.6 %reduce-scatter.5.cloned.1.call-done = bf16[128,896]{1,0:T(8,128)(2,1)} async-done(((bf16[4096,896]{1,0:T(8,128)(2,1)}), bf16[128,896]{1,0:T(8,128)(2,1)}) %reduce-scatter.5.cloned.1.call-update) | async-done | bytes 229392 | tf_op jit(solution)/shard_map/reduce_scatter | solution.py:67
  (26 shorter events, 0.6 us)
Async XLA Ops:
  6.5 276.1 %copy-start = (bf16[512,896]{1,0:T(8,128)(2,1)S(1)}, bf16[512,896]{1,0:T(8,128)(2,1)}, u32[]{:S(2)}) copy-start(bf16[512,896]{1,0:T(8,128)(2,1)} %param.13) | copy-start | bytes 2752516
  6.6 177.0 %all-gather.4.cloned.1.call-start = ((), (), s32[]{:S(2)}) async-start(), calls=%async_computation.2 | async-start | bytes 7569408 | tf_op jit(solution)/shard_map/all_gather | solution.py:44
  7.3 228.5 %reduce-scatter.3.cloned.1.call-start = ((), (), s32[]{:S(2)}) async-start(), calls=%async_computation.3 | async-start | bytes 4128768 | tf_op jit(solution)/shard_map/reduce_scatter | solution.py:52
  183.5 5.7 %copy-start.1 = (bf16[4096,896]{1,0:T(8,128)(2,1)S(1)}, bf16[4096,896]{1,0:T(8,128)(2,1)}, u32[]{:S(2)}) copy-start(bf16[4096,896]{1,0:T(8,128)(2,1)} %all-gather.4.cloned.1.call-done) | copy-start | bytes 22020100
  189.2 1.2 copy-start.4
  190.5 1.8 copy-start.5
  196.1 86.6 %all-gather.6.cloned.1.call-start = ((), (), s32[]{:S(2)}) async-start(), calls=%async_computation.4 | async-start | bytes 2064384 | tf_op jit(solution)/shard_map/all_gather | solution.py:58
  238.6 205.4 %reduce-scatter.5.cloned.1.call-start = ((), (), s32[]{:S(2)}) async-start(), calls=%async_computation.5 | async-start | bytes 7569408 | tf_op jit(solution)/shard_map/reduce_scatter | solution.py:67
  282.7 1.4 slice-start
  284.1 1.8 copy-start.2
  284.1 1.9 copy-start.3
Sparse Core Ops, SparseCore 0:
  9.4 174.0 all-gather.3
  196.2 39.5 reduce-scatter.2
  238.7 43.9 all-gather.5
  290.5 153.4 reduce-scatter.4
